TPU v7x, 32 devices: a whole 2x2x4 slice. The times are simulated.
32 devices in a mesh: row: 8 (over y, x, core), col: 4 (over z).
Axes of the slice: x: 2, y: 2, z: 4, core: 2. Of those that a mesh axis runs over, the one named last changes fastest.
Arguments:
- ctrl_start: float32 [16384, 512], P(('row', 'col')), may hold values from -6 to 6
- obsv_start: float32 [16384, 512], P(('row', 'col')), may hold values from -6 to 6
- band_tiles: float32 [16384, 384], P(('row', 'col')), may hold values from -0.15625 to 0.15625
- band_offsets: int32 [128, 3], P(('row', 'col')), may hold values from -2 to 2, as said below
Outputs:
- cross_product: float32 [2048, 2048], P('row', 'col')
Inputs may be any that keep to these rules, and one draw needn't show every extreme that they name: `band_offsets`: the 3 offsets of a tile row are distinct.
All inputs are finite; a program needn't handle non-finite values.
Results may differ from a plain program's by a relative error of at most 0.0003.
Values sent between devices are 32-bit elements; how exact they have to be, the bound alone decides.
No kernel may reach another device: no remote copies, remote signals or barrier semaphores. Data moves between devices by JAX's collectives and lax.ppermute only.
A program may use at most 128 MiB of HBM per device.

v0:
```python
import math

import jax
import jax.numpy as jnp
from jax import lax
from jax.sharding import PartitionSpec as P

TILE = 128
HALO = 2
BAND = 3


def extended(array, sides, width):
    for axis, dim in sides:
        size, length = (lax.axis_size(axis), array.shape[dim])
        up = [(i, (i + 1) % size) for i in range(size - 1)]
        down = [(j, i) for i, j in up]
        last = lax.slice_in_dim(array, length - width, length, axis=dim)
        initial = lax.slice_in_dim(array, 0, width, axis=dim)
        before = lax.ppermute(last, axis, up)
        after = lax.ppermute(initial, axis, down)
        array = jnp.concatenate([before, array, after], axis=dim)
    return array


def passed_along(array, axis, by):
    size = lax.axis_size(axis)
    pairs = [(i, i + by) for i in range(size) if 0 <= i + by < size]
    return lax.ppermute(array, axis, pairs)


def forward(field, tiles, offsets):
    margin = HALO * TILE
    padded = extended(field, ((("row", "col"), 0),), margin)
    results = []
    for index in range(field.shape[0] // TILE):
        parts = []
        for slot in range(BAND):
            start = (index + offsets[index, slot]) * TILE + margin
            parts.append(lax.dynamic_slice_in_dim(padded, start, TILE, 0))
        stacked = jnp.concatenate(parts, 0)
        results.append(
            jnp.dot(
                tiles[index * TILE : (index + 1) * TILE],
                stacked,
                precision=lax.Precision.HIGHEST,
                preferred_element_type=jnp.float32,
            )
        )
    return jnp.concatenate(results, 0)


def transpose(field, tiles, offsets):
    total = field.shape[0]
    margin = HALO * TILE
    padded = jnp.zeros((total + 2 * margin, field.shape[1]), jnp.float32)
    for index in range(total // TILE):
        piece = field[index * TILE : (index + 1) * TILE]
        terms = jnp.dot(
            tiles[index * TILE : (index + 1) * TILE].T,
            piece,
            precision=lax.Precision.HIGHEST,
            preferred_element_type=jnp.float32,
        )
        for slot in range(BAND):
            start = (index + offsets[index, slot]) * TILE + margin
            current = lax.dynamic_slice_in_dim(padded, start, TILE, 0)
            padded = lax.dynamic_update_slice_in_dim(
                padded, current + terms[slot * TILE : (slot + 1) * TILE], start, 0
            )
    lower = padded[:margin]
    upper = padded[total + margin :]
    middle = padded[margin : total + margin]
    from_above = passed_along(lower, ("row", "col"), -1)
    from_below = passed_along(upper, ("row", "col"), 1)
    middle = middle.at[:margin].add(from_below)
    middle = middle.at[total - margin :].add(from_above)
    return middle


def local(ctrl_start, obsv_start, band_tiles, band_offsets):
    ctrl_one = jnp.concatenate([ctrl_start, forward(ctrl_start, band_tiles, band_offsets)], 1)
    ctrl_two = jnp.concatenate(
        [ctrl_one, forward(forward(ctrl_one, band_tiles, band_offsets), band_tiles, band_offsets)],
        1,
    )
    obsv_one = jnp.concatenate([obsv_start, transpose(obsv_start, band_tiles, band_offsets)], 1)
    obsv_two = jnp.concatenate(
        [
            obsv_one,
            transpose(transpose(obsv_one, band_tiles, band_offsets), band_tiles, band_offsets),
        ],
        1,
    )
    rows_here = ctrl_two.shape[0]
    columns = ctrl_two.shape[1]
    row_count = lax.axis_size("row")
    col_count = lax.axis_size("col")
    left = obsv_two.reshape(rows_here, row_count, columns // row_count)
    right = ctrl_two.reshape(rows_here, col_count, columns // col_count)
    partial_sum = jnp.einsum(
        "nra,ncb->rcab",
        left,
        right,
        precision=lax.Precision.HIGHEST,
        preferred_element_type=jnp.float32,
    )
    partial_sum = partial_sum.reshape(
        row_count * col_count * (columns // row_count), columns // col_count
    )
    slab = lax.psum_scatter(partial_sum, "row", scatter_dimension=0, tiled=True)
    block = lax.psum_scatter(slab, "col", scatter_dimension=0, tiled=True)
    return block * (1.0 / math.sqrt(rows_here * row_count * col_count))


def solution(mesh):
    return jax.shard_map(
        local,
        mesh=mesh,
        in_specs=(
            P(("row", "col"), None),
            P(("row", "col"), None),
            P(("row", "col"), None),
            P(("row", "col"), None),
        ),
        out_specs=P("row", "col"),
        check_vma=False,
    )
```

profile of v0, /device:TPU:0, one launch (start us, length us, event | category | flops | bytes accessed | tf_op | source)
XLA Modules:
  0.0 503.5 jit_solution(12780872329202493021)
XLA Ops:
  6.5 1.8 fusion.193
  15.7 1.9 fusion.141
  17.6 2.8 fusion.143
  20.4 1.7 fusion.145
  25.0 5.1 %collective-permute-start.6 = (f32[256,512]{1,0:T(8,128)S(1)}, f32[256,512]{1,0:T(8,128)S(1)}, u32[]{:S(2)}, u32[]{:S(2)}) collective-permute-start(f32[256,512]{1,0:T(8,128)S(1)} %get-tuple-element.120), channel_id=1, source_target_pairs={{0,1},{1,2},{2,3},{3,4},{4,5},{5,6},{6,7},{7,8},{8,9},{9,10},{10,1... | collective-permute-start | bytes 1572872 | tf_op jit(solution)/shard_map/ppermute | solution.py:29
  30.2 1.3 collective-permute-start.7
  31.5 1.3 collective-permute-start.1
  32.8 5.7 %collective-permute-start = (f32[256,512]{1,0:T(8,128)S(1)}, f32[256,512]{1,0:T(8,128)S(1)}, u32[]{:S(2)}, u32[]{:S(2)}) collective-permute-start(f32[256,512]{1,0:T(8,128)S(1)} %get-tuple-element.122), channel_id=1, source_target_pairs={{0,1},{1,2},{2,3},{3,4},{4,5},{5,6},{6,7},{7,8},{8,9},{9,10},{10,1... | collective-permute-start | bytes 1572872 | tf_op jit(solution)/shard_map/ppermute | solution.py:20
  38.6 3.8 collective-permute-done.6
  42.5 13.7 %collective-permute-done.7 = f32[256,512]{1,0:T(8,128)S(1)} collective-permute-done((f32[256,512]{1,0:T(8,128)S(1)}, f32[256,512]{1,0:T(8,128)S(1)}, u32[]{:S(2)}, u32[]{:S(2)}) %collective-permute-start.7) | collective-permute-done | bytes 524320 | tf_op jit(solution)/shard_map/ppermute | solution.py:29
  56.4 1.4 convolution_bitcast_fusion.8
  57.8 1.4 convolution_bitcast_fusion.7
  59.4 1.4 convolution_bitcast_fusion.5
  60.8 1.4 convolution_bitcast_fusion.6
  62.3 5.6 %collective-permute-done.1 = f32[256,512]{1,0:T(8,128)S(1)} collective-permute-done((f32[256,512]{1,0:T(8,128)S(1)}, f32[256,512]{1,0:T(8,128)S(1)}, u32[]{:S(2)}, u32[]{:S(2)}) %collective-permute-start.1) | collective-permute-done | bytes 524320 | tf_op jit(solution)/shard_map/ppermute | solution.py:21
  71.7 1.4 fusion.190
  73.1 3.5 collective-permute-start.2
  80.3 2.0 copy-done.1
  83.4 1.5 collective-permute-start.9
  84.8 1.3 copy.8
  86.1 1.3 copy.9
  88.2 28.0 %collective-permute-done.3 = f32[256,1024]{1,0:T(8,128)} collective-permute-done((f32[256,1024]{1,0:T(8,128)}, f32[256,1024]{1,0:T(8,128)}, u32[]{:S(2)}, u32[]{:S(2)}) %collective-permute-start.3) | collective-permute-done | bytes 1048608 | tf_op jit(solution)/shard_map/ppermute | solution.py:21
  116.2 2.3 pad_maximum_fusion
  119.7 19.5 %collective-permute-done.9 = f32[256,1024]{0,1:T(8,128)} collective-permute-done((f32[256,1024]{0,1:T(8,128)}, f32[256,1024]{0,1:T(8,128)}, u32[]{:S(2)}, u32[]{:S(2)}) %collective-permute-start.9) | collective-permute-done | bytes 1048608 | tf_op jit(solution)/shard_map/ppermute | solution.py:29
  139.2 1.5 slice_add_fusion.2
  140.7 22.5 %collective-permute-start.8 = (f32[256,1024]{0,1:T(8,128)S(1)}, f32[256,1024]{0,1:T(8,128)S(1)}, u32[]{:S(2)}, u32[]{:S(2)}) collective-permute-start(f32[256,1024]{0,1:T(8,128)S(1)} %get-tuple-element.104), channel_id=1, source_target_pairs={{0,1},{1,2},{2,3},{3,4},{4,5},{5,6},{6,7},{7,8},{8,9},{9,10},{10,1... | collective-permute-start | bytes 3145736 | tf_op jit(solution)/shard_map/ppermute | solution.py:29
  165.7 2.6 collective-permute-start.4
  168.3 1.4 convolution_bitcast_fusion.1
  169.7 1.4 convolution_bitcast_fusion.2
  171.1 15.6 %collective-permute-done.8 = f32[256,1024]{0,1:T(8,128)S(1)} collective-permute-done((f32[256,1024]{0,1:T(8,128)S(1)}, f32[256,1024]{0,1:T(8,128)S(1)}, u32[]{:S(2)}, u32[]{:S(2)}) %collective-permute-start.8) | collective-permute-done | bytes 1048608 | tf_op jit(solution)/shard_map/ppermute | solution.py:29
  187.0 1.4 convolution_bitcast_fusion.3
  188.4 1.4 convolution_bitcast_fusion.4
  189.8 18.3 %collective-permute-done.4 = f32[256,1024]{1,0:T(8,128)S(1)} collective-permute-done((f32[256,1024]{1,0:T(8,128)S(1)}, f32[256,1024]{1,0:T(8,128)S(1)}, u32[]{:S(2)}, u32[]{:S(2)}) %collective-permute-start.4) | collective-permute-done | bytes 1048608 | tf_op jit(solution)/shard_map/ppermute | solution.py:20
  210.6 1.3 collective-permute-start.5
  214.3 1.7 slice.574
  216.9 1.5 fusion.189
  219.7 6.8 %collective-permute-start.10 = (f32[256,1024]{0,1:T(8,128)}, f32[256,1024]{0,1:T(8,128)}, u32[]{:S(2)}, u32[]{:S(2)}) collective-permute-start(f32[256,1024]{0,1:T(8,128)} %get-tuple-element.102), channel_id=1, source_target_pairs={{0,1},{1,2},{2,3},{3,4},{4,5},{5,6},{6,7},{7,8},{8,9},{9,10},{10,1... | collective-permute-start | bytes 3145736 | tf_op jit(solution)/shard_map/ppermute | solution.py:29
  226.6 12.4 %collective-permute-done.5 = f32[256,1024]{1,0:T(8,128)S(1)} collective-permute-done((f32[256,1024]{1,0:T(8,128)S(1)}, f32[256,1024]{1,0:T(8,128)S(1)}, u32[]{:S(2)}, u32[]{:S(2)}) %collective-permute-start.5) | collective-permute-done | bytes 1048608 | tf_op jit(solution)/shard_map/ppermute | solution.py:21
  244.4 6.1 %maximum_maximum_fusion = f32[512,2048]{1,0:T(8,128)} fusion(f32[128,1024]{1,0:T(8,128)S(1)} %fusion.49, f32[128,1024]{1,0:T(8,128)S(1)} %fusion.52, f32[128,1024]{1,0:T(8,128)S(1)} %fusion.55, f32[128,1024]{1,0:T(8,128)S(1)} %fusion.58, f32[128,512]{1,0:T(8,128)S(1)} %convolution_bitcast_fusion.9, f32[128,512]{1,0:T(8,128)S(1)} %copy-done.9, ...), kind=kLoop, calls=%fused_computation.2 | loop fusion | flops 8388608 | bytes 8388608 | tf_op jit(solution)/shard_map/concatenate | solution.py:83
  250.4 6.0 %reshape.240 = f32[512,4,512]{2,1,0:T(4,128)} reshape(f32[512,2048]{1,0:T(8,128)} %maximum_maximum_fusion) | data formatting | bytes 8388608 | tf_op jit(solution)/shard_map/reshape | solution.py:100
  256.5 2.7 fusion.74
  260.2 2.4 fusion.73
  262.6 2.2 pad_maximum_fusion.1
  265.4 32.8 %convolution_bitcast_fusion = f32[8,4,256,512]{3,2,0,1:T(8,128)S(1)} fusion(f32[512,8,256,1]{0,2,1,3:T(8,128)S(1)} %bitcast.73, f32[512,4,512,1]{2,1,0,3:T(4,128)S(1)} %bitcast.74), kind=kOutput, calls=%fused_computation | convolution fusion | flops 25769803776 | bytes 25165824 | tf_op jit(solution)/shard_map/nra,ncb->rcab/dot_general | solution.py:101
  298.2 6.2 %copy.11 = f32[8,4,256,512]{3,2,1,0:T(8,128)} copy(f32[8,4,256,512]{3,2,0,1:T(8,128)S(1)} %convolution_bitcast_fusion) | data formatting | bytes 33554432 | tf_op jit(solution)/shard_map/nra,ncb->rcab/transpose | solution.py:101
  304.5 144.0 %reduce-scatter.3.cloned.1.call-done = f32[1024,512]{1,0:T(8,128)} async-done(((f32[8192,512]{1,0:T(8,128)}), f32[1024,512]{1,0:T(8,128)}) %reduce-scatter.3.cloned.1.call-update) | async-done | bytes 2097168 | tf_op jit(solution)/shard_map/reduce_scatter | solution.py:111
  448.5 45.9 %reduce-scatter.5.cloned.1.call-done = f32[256,512]{1,0:T(8,128)} async-done(((f32[1024,512]{1,0:T(8,128)}), f32[256,512]{1,0:T(8,128)}) %reduce-scatter.5.cloned.1.call-update) | async-done | bytes 524304 | tf_op jit(solution)/shard_map/reduce_scatter | solution.py:112
  494.4 1.9 broadcast_multiply_fusion
  (113 shorter events, 30.3 us)
Async XLA Ops:
  6.5 13.9 %copy-start.4 = (f32[512,384]{1,0:T(8,128)S(1)}, f32[512,384]{1,0:T(8,128)}, u32[]{:S(2)}) copy-start(f32[512,384]{1,0:T(8,128)} %param.18) | copy-start | bytes 2359300
  6.5 13.9 %copy-start.3 = (f32[512,512]{1,0:T(8,128)S(1)}, f32[512,512]{1,0:T(8,128)}, u32[]{:S(2)}) copy-start(f32[512,512]{1,0:T(8,128)} %param.17) | copy-start | bytes 3145732
  6.5 442.0 %reduce-scatter.3.cloned.1.call-start = ((), (), s32[]{:S(2)}) async-start(), calls=%async_computation.2 | async-start | bytes 18874368 | tf_op jit(solution)/shard_map/reduce_scatter | solution.py:111
  23.1 1.1 copy-start.15
  23.4 1.2 copy-start.14
  24.7 6.7 %copy-start.5 = (f32[512,512]{1,0:T(8,128)S(1)}, f32[512,512]{1,0:T(8,128)}, u32[]{:S(2)}) copy-start(f32[512,512]{1,0:T(8,128)} %param.16) | copy-start | bytes 3145732
  25.0 17.4 %collective-permute-start.6 = (f32[256,512]{1,0:T(8,128)S(1)}, f32[256,512]{1,0:T(8,128)S(1)}, u32[]{:S(2)}, u32[]{:S(2)}) collective-permute-start(f32[256,512]{1,0:T(8,128)S(1)} %get-tuple-element.120), channel_id=1, source_target_pairs={{0,1},{1,2},{2,3},{3,4},{4,5},{5,6},{6,7},{7,8},{8,9},{9,10},{10,1... | collective-permute-start | bytes 1572872 | tf_op jit(solution)/shard_map/ppermute | solution.py:29
  30.2 26.1 %collective-permute-start.7 = (f32[256,512]{1,0:T(8,128)S(1)}, f32[256,512]{1,0:T(8,128)S(1)}, u32[]{:S(2)}, u32[]{:S(2)}) collective-permute-start(f32[256,512]{1,0:T(8,128)S(1)} %get-tuple-element.119), channel_id=1, source_target_pairs={{1,0},{2,1},{3,2},{4,3},{5,4},{6,5},{7,6},{8,7},{9,8},{10,9},{11,1... | collective-permute-start | bytes 1572872 | tf_op jit(solution)/shard_map/ppermute | solution.py:29
  31.5 36.4 %collective-permute-start.1 = (f32[256,512]{1,0:T(8,128)S(1)}, f32[256,512]{1,0:T(8,128)S(1)}, u32[]{:S(2)}, u32[]{:S(2)}) collective-permute-start(f32[256,512]{1,0:T(8,128)S(1)} %get-tuple-element.121), channel_id=1, source_target_pairs={{1,0},{2,1},{3,2},{4,3},{5,4},{6,5},{7,6},{8,7},{9,8},{10,9},{11,1... | collective-permute-start | bytes 1572872 | tf_op jit(solution)/shard_map/ppermute | solution.py:21
  32.8 26.4 %collective-permute-start = (f32[256,512]{1,0:T(8,128)S(1)}, f32[256,512]{1,0:T(8,128)S(1)}, u32[]{:S(2)}, u32[]{:S(2)}) collective-permute-start(f32[256,512]{1,0:T(8,128)S(1)} %get-tuple-element.122), channel_id=1, source_target_pairs={{0,1},{1,2},{2,3},{3,4},{4,5},{5,6},{6,7},{7,8},{8,9},{9,10},{10,1... | collective-permute-start | bytes 1572872 | tf_op jit(solution)/shard_map/ppermute | solution.py:20
  70.3 0.9 copy-start.8
  70.9 0.7 copy-start.10
  73.1 15.1 %collective-permute-start.2 = (f32[256,1024]{1,0:T(8,128)}, f32[256,1024]{1,0:T(8,128)}, u32[]{:S(2)}, u32[]{:S(2)}) collective-permute-start(f32[256,1024]{1,0:T(8,128)} %get-tuple-element.105), channel_id=1, source_target_pairs={{0,1},{1,2},{2,3},{3,4},{4,5},{5,6},{6,7},{7,8},{8,9},{9,10},{10,1... | collective-permute-start | bytes 3145736 | tf_op jit(solution)/shard_map/ppermute | solution.py:20
  76.6 39.7 %collective-permute-start.3 = (f32[256,1024]{1,0:T(8,128)}, f32[256,1024]{1,0:T(8,128)}, u32[]{:S(2)}, u32[]{:S(2)}) collective-permute-start(f32[256,1024]{1,0:T(8,128)} %get-tuple-element.106), channel_id=1, source_target_pairs={{1,0},{2,1},{3,2},{4,3},{5,4},{6,5},{7,6},{8,7},{9,8},{10,9},{11,1... | collective-permute-start | bytes 3145736 | tf_op jit(solution)/shard_map/ppermute | solution.py:21
  80.3 2.0 copy-start.1
  83.4 55.8 %collective-permute-start.9 = (f32[256,1024]{0,1:T(8,128)}, f32[256,1024]{0,1:T(8,128)}, u32[]{:S(2)}, u32[]{:S(2)}) collective-permute-start(f32[256,1024]{0,1:T(8,128)} %slice.565), channel_id=1, source_target_pairs={{1,0},{2,1},{3,2},{4,3},{5,4},{6,5},{7,6},{8,7},{9,8},{10,9},{11,1... | collective-permute-start | bytes 3145736 | tf_op jit(solution)/shard_map/ppermute | solution.py:29
  86.1 30.1 %copy-start.6 = (f32[512,512]{1,0:T(8,128)S(1)}, f32[512,512]{1,0:T(8,128)}, u32[]{:S(2)}) copy-start(f32[512,512]{1,0:T(8,128)} %param.16) | copy-start | bytes 3145732
  118.6 20.6 %copy-start.2 = (f32[1024,1024]{0,1:T(8,128)S(1)}, f32[1024,1024]{0,1:T(8,128)}, u32[]{:S(2)}) copy-start(f32[1024,1024]{0,1:T(8,128)} %copy-done.1) | copy-start | bytes 12582916
  140.7 46.0 %collective-permute-start.8 = (f32[256,1024]{0,1:T(8,128)S(1)}, f32[256,1024]{0,1:T(8,128)S(1)}, u32[]{:S(2)}, u32[]{:S(2)}) collective-permute-start(f32[256,1024]{0,1:T(8,128)S(1)} %get-tuple-element.104), channel_id=1, source_target_pairs={{0,1},{1,2},{2,3},{3,4},{4,5},{5,6},{6,7},{7,8},{8,9},{9,10},{10,1... | collective-permute-start | bytes 3145736 | tf_op jit(solution)/shard_map/ppermute | solution.py:29
  165.7 42.4 %collective-permute-start.4 = (f32[256,1024]{1,0:T(8,128)S(1)}, f32[256,1024]{1,0:T(8,128)S(1)}, u32[]{:S(2)}, u32[]{:S(2)}) collective-permute-start(f32[256,1024]{1,0:T(8,128)S(1)} %pad_maximum_fusion.2), channel_id=1, source_target_pairs={{0,1},{1,2},{2,3},{3,4},{4,5},{5,6},{6,7},{7,8},{8,9},{9,10},{10,1... | collective-permute-start | bytes 3145736 | tf_op jit(solution)/shard_map/ppermute | solution.py:20
  210.6 28.4 %collective-permute-start.5 = (f32[256,1024]{1,0:T(8,128)S(1)}, f32[256,1024]{1,0:T(8,128)S(1)}, u32[]{:S(2)}, u32[]{:S(2)}) collective-permute-start(f32[256,1024]{1,0:T(8,128)S(1)} %pad_maximum_fusion.3), channel_id=1, source_target_pairs={{1,0},{2,1},{3,2},{4,3},{5,4},{6,5},{7,6},{8,7},{9,8},{10,9},{11,1... | collective-permute-start | bytes 3145736 | tf_op jit(solution)/shard_map/ppermute | solution.py:21
  214.3 2.7 copy-start
  218.4 41.8 %collective-permute-start.11 = (f32[256,1024]{0,1:T(8,128)}, f32[256,1024]{0,1:T(8,128)S(1)}, u32[]{:S(2)}, u32[]{:S(2)}) collective-permute-start(f32[256,1024]{0,1:T(8,128)} %get-tuple-element.101), channel_id=1, source_target_pairs={{1,0},{2,1},{3,2},{4,3},{5,4},{6,5},{7,6},{8,7},{9,8},{10,9},{11,1... | collective-permute-start | bytes 3145736 | tf_op jit(solution)/shard_map/ppermute | solution.py:29
  219.7 36.8 %collective-permute-start.10 = (f32[256,1024]{0,1:T(8,128)}, f32[256,1024]{0,1:T(8,128)}, u32[]{:S(2)}, u32[]{:S(2)}) collective-permute-start(f32[256,1024]{0,1:T(8,128)} %get-tuple-element.102), channel_id=1, source_target_pairs={{0,1},{1,2},{2,3},{3,4},{4,5},{5,6},{6,7},{7,8},{8,9},{9,10},{10,1... | collective-permute-start | bytes 3145736 | tf_op jit(solution)/shard_map/ppermute | solution.py:29
  242.0 2.4 copy-start.9
  242.0 2.4 copy-start.11
  259.2 3.4 copy-start.12
  259.2 3.4 copy-start.13
  262.6 2.8 copy-start.7
  304.5 190.0 %reduce-scatter.5.cloned.1.call-start = ((), (), s32[]{:S(2)}) async-start(), calls=%async_computation.3 | async-start | bytes 2621440 | tf_op jit(solution)/shard_map/reduce_scatter | solution.py:112
Sparse Core Ops, SparseCore 0:
  304.6 143.8 reduce-scatter.2
  450.8 43.5 reduce-scatter.4
where the time goes:
time: 508 us; the launch traced here: 504 us
  waiting for transfers between devices  309 us (61%)
  matrix products  63.2 us (12%)
  starting transfers between devices  54.1 us (11%)
  local copies, waits for them, and re-layouts  31.4 us (6%)
  other arithmetic  24 us (5%)
  between operations  22.1 us (4%)
    reduce_scatter x1, waiting for transfers between devices, local(): slab = lax.psum_scatter(partial_sum, 'row', scatter_dimension=0, tiled=True)  144 us
    ppermute x6, waiting for transfers between devices, passed_along(): return lax.ppermute(array, axis, pairs)  53.7 us
    ppermute x3, waiting for transfers between devices, extended(): after = lax.ppermute(initial, axis, down)  46 us
    reduce_scatter x1, waiting for transfers between devices, local(): block = lax.psum_scatter(slab, 'col', scatter_dimension=0, tiled=True)  45.9 us
    ppermute x6, starting transfers between devices, passed_along(): return lax.ppermute(array, axis, pairs)  38.5 us
    dot_general x1, matrix products, local(): jnp.einsum('nra,ncb->rcab', left, right, precision=lax.Precision.HIGHEST,...  32.8 us
    ppermute x3, waiting for transfers between devices, extended(): before = lax.ppermute(last, axis, up)  19 us
    dot_general x12, matrix products, transpose(): jnp.dot(tiles[index * TILE:(index + 1) * TILE].T, piece, precision=lax.Pr...  18.5 us
  transfers between devices with their start and end apart: 14, of which 12 were waited for; matrix products, arithmetic and copies ran while one was open for 10% of the time, Pallas kernels for 0%

commit v1 on v0

v1 whole, which is shorter than its diff:
```python
import functools
import math

import jax
import jax.numpy as jnp
from jax import lax
from jax.experimental import pallas as pl
from jax.experimental.pallas import tpu as pltpu
from jax.sharding import PartitionSpec as P

TILE = 128
HALO = 2
BAND = 3
ORDERS = 4
AXES = ("row", "col")
VMEM = pltpu.VMEM
GROUPS = ((0, 1, 2), (3, 4, 5), (6,))


def call(kernel, outs, ins, scratch=(), flops=0, bytes_=0, scalars=0):
    specs = [pl.BlockSpec(memory_space=pltpu.SMEM)] * scalars
    specs += [pl.BlockSpec(memory_space=VMEM)] * (len(ins) - scalars)
    return pl.pallas_call(
        kernel,
        out_shape=outs,
        in_specs=specs,
        out_specs=jax.tree.map(lambda _: pl.BlockSpec(memory_space=VMEM), outs),
        scratch_shapes=list(scratch),
        cost_estimate=pl.CostEstimate(flops=flops, bytes_accessed=bytes_, transcendentals=0),
    )(*ins)


def split(value):
    high = value.astype(jnp.bfloat16)
    return high, (value - high.astype(jnp.float32)).astype(jnp.bfloat16)


def dot(a, b):
    return jnp.dot(a, b, preferred_element_type=jnp.float32)


def forward_kernel(offs, before, top, bottom, after, tiles, top_out, bottom_out, high, low):
    margin = HALO * TILE
    for place, ref in enumerate((before, top, bottom, after)):
        here = pl.ds(place * margin, margin)
        high[here, :], low[here, :] = split(ref[...])
    for index in range(2 * HALO):
        starts = [pl.multiple_of((index + HALO + offs[index, b]) * TILE, TILE) for b in range(BAND)]
        stack_high = jnp.concatenate([high[pl.ds(s, TILE), :] for s in starts], 0)
        stack_low = jnp.concatenate([low[pl.ds(s, TILE), :] for s in starts], 0)
        tile_high, tile_low = split(tiles[index * TILE : (index + 1) * TILE, :])
        result = dot(tile_high, stack_high) + (dot(tile_high, stack_low) + dot(tile_low, stack_high))
        out, at = (top_out, index) if index < HALO else (bottom_out, index - HALO)
        out[at * TILE : (at + 1) * TILE, :] = result


def forward(offs, before, top, bottom, after, tiles):
    shape = jax.ShapeDtypeStruct(top.shape, jnp.float32)
    rows, width = 2 * top.shape[0], top.shape[1]
    scratch = [VMEM((2 * rows, width), jnp.bfloat16)] * 2
    return call(
        forward_kernel, (shape, shape), (offs, before, top, bottom, after, tiles), scratch,
        6 * rows * BAND * TILE * width, 4 * (4 * rows * width), 1,
    )


def turn_kernel(parts, quarters, pos, obsv, high_out, low_out):
    high, low = split(obsv[...].T)
    width = high.shape[0] // (parts * quarters)
    for d in range(parts):
        for e in range(quarters):
            for p in range(parts):
                for q in range(quarters):
                    @pl.when(jnp.logical_and((pos[0] + d) % parts == p, (pos[1] + e) % quarters == q))
                    def _(d=d, e=e, p=p, q=q):
                        here = (d * quarters + e) * width
                        there = (p * quarters + q) * width
                        high_out[here : here + width, :] = high[there : there + width]
                        low_out[here : here + width, :] = low[there : there + width]


def product_kernel(high, low, top, bottom, *outs):
    half = top.shape[0]
    right_high, right_low = split(jnp.concatenate([top[...], bottom[...]], 0))
    rows = high.shape[0] // len(outs)
    for d, out in enumerate(outs):
        here = pl.ds(d * rows, rows)
        a = high[here, :]
        out[...] = dot(a, right_high) + (dot(a, right_low) + dot(low[here, :], right_high))


def product(high, low, top, bottom, parts):
    rows, width = high.shape[0], top.shape[1]
    shapes = tuple(jax.ShapeDtypeStruct((rows // parts, width), jnp.float32) for _ in range(parts))
    return call(
        product_kernel, shapes, (high, low, top, bottom), (),
        6 * rows * width * high.shape[1], 4 * 4 * rows * width,
    )


def pick_kernel(count, pos, *refs):
    sources, outs = refs[: -count], refs[-count:]
    for d, out in enumerate(outs):
        power = (pos[1] + d) % count + pos[2]
        for k, ref in enumerate(sources):
            @pl.when(power == k)
            def _(out=out, ref=ref):
                out[...] = ref[...]


def place_kernel(scale, pos, *refs):
    *parts, out = refs
    count = len(parts)
    rows = parts[0].shape[0]
    for d, ref in enumerate(parts):
        at = (pos[1] + count - d) % count
        out[pl.ds(pl.multiple_of(at * rows, rows), rows), :] = ref[...] * scale


def local(rows_all, cols_all, ctrl, obsv, tiles, offs):
    total = rows_all * cols_all
    parts, splits = rows_all // ORDERS, cols_all // ORDERS
    r, c = lax.axis_index("row"), lax.axis_index("col")
    big_row, part, big_col, piece = r // parts, r % parts, c // splits, c % splits
    pos = jnp.stack([part, big_row, big_col, piece]).astype(jnp.int32)
    devices = [(i, j) for i in range(rows_all) for j in range(cols_all)]

    def flat(i, j):
        return i * cols_all + j

    def permute(x, pairs):
        return lax.ppermute(x, AXES, pairs)

    def peers(move):
        return [(flat(i, j), flat(*move(i, j))) for i, j in devices]

    def seat(s):
        lane, q = divmod(s, 2 * cols_all)
        j = q // 2 if lane % 2 == 0 else cols_all - 1 - q // 2
        return flat(2 * lane + q % 2, j)

    seats = [seat(s) for s in range(total)]
    relay = [(s, seats[s]) for s in range(total)]
    up = [(seats[s], seats[s + 1]) for s in range(total - 1)]
    down = [(b, a) for a, b in up]

    margin = HALO * TILE
    width = ctrl.shape[1]
    offs = permute(offs, relay)
    top, bottom = permute(ctrl[:margin], relay), permute(ctrl[margin:], relay)
    tiles = permute(tiles, relay)
    obsv = permute(obsv, relay)
    quarter = width // (parts * ORDERS)
    half = jax.ShapeDtypeStruct((width, obsv.shape[0]), jnp.bfloat16)
    high, low = call(
        functools.partial(turn_kernel, parts, ORDERS), (half, half), (pos, obsv), (),
        width * width, 8 * width * width, 1,
    )

    def over_parts(blocks):
        kept = blocks[0]
        for d in range(1, parts):
            kept = kept + permute(
                blocks[d], peers(lambda i, j: ((i // parts) * parts + (i + d) % parts, j))
            )
        if splits == 1:
            return kept
        wide = kept.shape[1] // splits
        cut = [
            lax.dynamic_slice_in_dim(kept, ((piece + d) % splits) * wide, wide, 1)
            for d in range(splits)
        ]
        kept = cut[0]
        for d in range(1, splits):
            kept = kept + permute(
                cut[d], peers(lambda i, j: (i, (j // splits) * splits + (j + d) % splits))
            )
        return kept

    def turned(i, e):
        return ((i // parts + e) % ORDERS) * parts + i % parts

    def over_rows(block):
        kept = block[:, :quarter]
        for e in range(1, ORDERS):
            sent = block[:, e * quarter : (e + 1) * quarter]
            kept = kept + permute(sent, peers(lambda i, j: (turned(i, e), j)))
        return kept

    def line(moves):
        return [
            (flat(i, a * splits + s), flat(i, b * splits + s))
            for a, b in moves for i in range(rows_all) for s in range(splits)
        ]

    def over_cols(own, powers):
        low_k, high_k = min(powers), max(powers)
        last = 2 * ORDERS - 2
        first = []
        if high_k >= 1:
            first.append((0, 1))
        if low_k < last:
            first.append((3, 2))
        second = []
        if high_k >= 2:
            second.append((1, 2))
        if low_k <= last - 2:
            second.append((2, 1))
        third = []
        if low_k <= ORDERS - 1:
            third.append((1, 0))
        if high_k >= ORDERS - 1:
            third.append((2, 3))
        both = own + permute(own, line(first))
        both = both + permute(both, line(second))
        ends = permute(both, line(third))
        if (3, 2) not in first:
            ends = ends + jnp.where(big_col == 3, own, 0.0)
        outer = jnp.logical_or(big_col == 0, big_col == 3)
        return jnp.where(outer, ends, both)

    powers = {}
    kept = {}
    for group in GROUPS:
        sums = []
        for k in group:
            if k > 0:
                before, after = permute(bottom, up), permute(top, down)
                top, bottom = forward(offs, before, top, bottom, after, tiles)
            sums.append(over_parts(product(high, low, top, bottom, parts)))
        own = over_rows(jnp.stack(sums))
        done = over_cols(own, group)
        for at, k in enumerate(group):
            kept[k] = done[at]

    shape = kept[0].shape
    block = jax.ShapeDtypeStruct(shape, jnp.float32)
    sent = call(
        functools.partial(pick_kernel, ORDERS), (block,) * ORDERS,
        (pos, *[kept[k] for k in range(2 * ORDERS - 1)]), (), shape[0] * shape[1], 44 * shape[0] * shape[1], 1,
    )
    got = [sent[0]] + [permute(sent[d], peers(lambda i, j: (turned(i, d), j))) for d in range(1, ORDERS)]
    out = jax.ShapeDtypeStruct((ORDERS * shape[0], shape[1]), jnp.float32)
    scale = 1.0 / math.sqrt(ctrl.shape[0] * total)
    return call(
        functools.partial(place_kernel, scale), out, (pos, *got), (),
        shape[0] * shape[1], 32 * shape[0] * shape[1], 1,
    )


def solution(mesh):
    return jax.shard_map(
        functools.partial(local, mesh.shape["row"], mesh.shape["col"]),
        mesh=mesh,
        in_specs=(P(AXES, None),) * 4,
        out_specs=P("row", "col"),
        check_vma=False,
    )
```

time: 508 us -> 260 us (0.51)
  waiting for transfers between devices: 309 us -> 48 us
  starting transfers between devices: 54.1 us -> 138 us
  matrix products: 63.2 us -> 0 us
  Pallas kernels: 0 us -> 55.3 us
  local copies, waits for them, and re-layouts: 31.4 us -> 9.84 us
  between operations: 22.1 us -> 0.69 us
  other arithmetic: 24 us -> 6.41 us
    reduce_scatter x2 -> x0, waiting for transfers between devices: 190 us -> none  [the longest x1 144 us: local(): slab = lax.psum_scatter(partial_sum, 'row', scatter_dimension=0, tiled=True)]
    ppermute x12 -> x45, starting transfers between devices: 54.1 us -> 138 us  [permute(): return lax.ppermute(x, AXES, pairs)]
    ppermute x12 -> x45, waiting for transfers between devices: 119 us -> 48 us  [permute(): return lax.ppermute(x, AXES, pairs)]
    dot_general x25 -> x0, matrix products: 63.2 us -> none  [the longest x1 32.8 us: local(): jnp.einsum('nra,ncb->rcab', left, right, precision=lax.Precision.HIGHEST,...]
    pallas_call x0 -> x16, Pallas kernels: none -> 55.3 us  [call(): pl.pallas_call(kernel, out_shape=outs, in_specs=specs, out_specs=jax.tree...]
    concatenate x6 -> x0, other arithmetic: 10.9 us -> none  [the longest x1 6.06 us: local(): jnp.concatenate([ctrl_one, forward(forward(ctrl_one, band_tiles, band_off...]
    transpose x1 -> x0, local copies, waits for them, and re-layouts: 6.21 us -> none  [local(): jnp.einsum('nra,ncb->rcab', left, right, precision=lax.Precision.HIGHEST,...]
    reshape x1 -> x0, local copies, waits for them, and re-layouts: 6.04 us -> none  [local(): right = ctrl_two.reshape(rows_here, col_count, columns // col_count)]
  transfers between devices with their start and end apart: 14 -> 45, of which waited for: 12 -> 10; matrix products, arithmetic and copies ran while one was open for 10% -> 3% of each run, Pallas kernels for 0% -> 18%
where the time goes in v1:
time: 260 us; the launch traced here: 258 us
  starting transfers between devices  138 us (53%)
  Pallas kernels  55.3 us (21%)
  waiting for transfers between devices  48 us (18%)
  local copies, waits for them, and re-layouts  9.84 us (4%)
  other arithmetic  6.41 us (2%)
    ppermute x45, starting transfers between devices, permute(): return lax.ppermute(x, AXES, pairs)  138 us
    pallas_call x16, Pallas kernels, call(): pl.pallas_call(kernel, out_shape=outs, in_specs=specs, out_specs=jax.tree...  55.3 us
    ppermute x45, waiting for transfers between devices, permute(): return lax.ppermute(x, AXES, pairs)  48 us
  transfers between devices with their start and end apart: 45, of which 10 were waited for; matrix products, arithmetic and copies ran while one was open for 3% of the time, Pallas kernels for 18%

profile of v1, /device:TPU:0, one launch (start us, length us, event | category | flops | bytes accessed | tf_op | source)
XLA Modules:
  0.0 258.5 jit_solution(16214463945931698251)
XLA Ops:
  0.0 1.3 fusion.8
  3.5 12.0 %collective-permute-start.5 = (f32[256,512]{1,0:T(8,128)S(1)}, f32[256,512]{1,0:T(8,128)S(1)}, u32[]{:S(2)}, u32[]{:S(2)}) collective-permute-start(f32[256,512]{1,0:T(8,128)S(1)} %collective-permute-done.2.bottom), channel_id=1, source_target_pairs={{0,4},{4,1},{1,5},{5,2},{2,6},{6,3},{3,7},{7,11},{11,15},{15,10},{... | collective-permute-start | bytes 1572872 | tf_op jit(solution)/shard_map/ppermute | solution.py:132
  16.9 1.9 collective-permute-start
  19.5 21.2 %collective-permute-done.6.after = f32[256,512]{1,0:T(8,128)} collective-permute-done((f32[256,512]{1,0:T(8,128)S(1)}, f32[256,512]{1,0:T(8,128)}, u32[]{:S(2)}, u32[]{:S(2)}) %collective-permute-start.6) | collective-permute-done | bytes 524320 | tf_op jit(solution)/shard_map/ppermute | solution.py:132
  40.7 4.1 %shard_map.48 = (f32[256,512]{1,0:T(8,128)}, f32[256,512]{1,0:T(8,128)}) custom-call(s32[4,3]{1,0:T(4,128)} %copy-done.21, f32[256,512]{1,0:T(8,128)} %copy-done.17, f32[256,512]{1,0:T(8,128)} %copy-done.3, f32[256,512]{1,0:T(8,128)} %copy-done.2, f32[256,512]{1,0:T(8,128)} %collective-permute-done.6.after, f32[512,384]{1,0:T(8,128)} %copy-done), custom_call_target="tpu_custom_call" | custom-call | flops 603979776 | bytes 4194304 | tf_op jit(solution)/shard_map/pallas_call | solution.py:23
  46.0 23.9 %collective-permute-start.9 = (f32[256,512]{1,0:T(8,128)}, f32[256,512]{1,0:T(8,128)S(1)}, u32[]{:S(2)}, u32[]{:S(2)}) collective-permute-start(f32[256,512]{1,0:T(8,128)} %get-tuple-element.42.bottom), channel_id=1, source_target_pairs={{0,4},{4,1},{1,5},{5,2},{2,6},{6,3},{3,7},{7,11},{11,15},{15,10},{... | collective-permute-start | bytes 1572872 | tf_op jit(solution)/shard_map/ppermute | solution.py:132
  71.5 3.5 %shard_map.46 = (bf16[512,512]{1,0:T(8,128)(2,1)}, bf16[512,512]{1,0:T(8,128)(2,1)}) custom-call(s32[4]{0:T(128)} %pad_add_fusion.pos, f32[512,512]{1,0:T(8,128)} %copy-done.1), custom_call_target="tpu_custom_call" | custom-call | flops 262144 | bytes 2097152 | tf_op jit(solution)/shard_map/pallas_call | solution.py:23
  76.6 4.0 %shard_map.50 = (f32[256,512]{1,0:T(8,128)}, f32[256,512]{1,0:T(8,128)}) custom-call(s32[4,3]{1,0:T(4,128)} %copy-done.21, f32[256,512]{1,0:T(8,128)} %copy-done.8, f32[256,512]{1,0:T(8,128)} %get-tuple-element.41.top, f32[256,512]{1,0:T(8,128)} %get-tuple-element.42.bottom, f32[256,512]{1,0:T(8,128)} %copy-done.6, f32[512,384]{1,0:T(8,128)} %copy-done), custom_call_target="tpu_custom_call" | custom-call | flops 603979776 | bytes 4194304 | tf_op jit(solution)/shard_map/pallas_call | solution.py:23
  80.7 18.9 %collective-permute-start.18 = (f32[256,512]{1,0:T(8,128)}, f32[256,512]{1,0:T(8,128)S(1)}, u32[]{:S(2)}, u32[]{:S(2)}) collective-permute-start(f32[256,512]{1,0:T(8,128)} %get-tuple-element.46.bottom), channel_id=1, source_target_pairs={{0,4},{4,1},{1,5},{5,2},{2,6},{6,3},{3,7},{7,11},{11,15},{15,10},{... | collective-permute-start | bytes 1572872 | tf_op jit(solution)/shard_map/ppermute | solution.py:132
  99.6 1.3 collective-permute-start.19
  100.9 3.3 %shard_map.49 = (f32[256,512]{1,0:T(8,128)}, f32[256,512]{1,0:T(8,128)}) custom-call(bf16[512,512]{1,0:T(8,128)(2,1)} %get-tuple-element.37.high, bf16[512,512]{1,0:T(8,128)(2,1)} %get-tuple-element.38.low, f32[256,512]{1,0:T(8,128)} %get-tuple-element.41.top, f32[256,512]{1,0:T(8,128)} %get-tuple-element.42.bottom), custom_call_target="tpu_custom_call" | custom-call | flops 805306368 | bytes 4194304 | tf_op jit(solution)/shard_map/pallas_call | solution.py:23
  104.2 3.0 %collective-permute-start.8 = (f32[256,512]{1,0:T(8,128)}, f32[256,512]{1,0:T(8,128)S(1)}, u32[]{:S(2)}, u32[]{:S(2)}) collective-permute-start(f32[256,512]{1,0:T(8,128)} %get-tuple-element.44), channel_id=1, source_target_pairs={{0,4},{1,5},{2,6},{3,7},{4,0},{5,1},{6,2},{7,3},{8,12},{9,13},{10,... | collective-permute-start | bytes 1572872 | tf_op jit(solution)/shard_map/ppermute | solution.py:132
  107.2 3.3 %shard_map.47 = (f32[256,512]{1,0:T(8,128)}, f32[256,512]{1,0:T(8,128)}) custom-call(bf16[512,512]{1,0:T(8,128)(2,1)} %get-tuple-element.37.high, bf16[512,512]{1,0:T(8,128)(2,1)} %get-tuple-element.38.low, f32[256,512]{1,0:T(8,128)} %copy-done.3, f32[256,512]{1,0:T(8,128)} %copy-done.2), custom_call_target="tpu_custom_call" | custom-call | flops 805306368 | bytes 4194304 | tf_op jit(solution)/shard_map/pallas_call | solution.py:23
  110.5 3.3 %shard_map.51 = (f32[256,512]{1,0:T(8,128)}, f32[256,512]{1,0:T(8,128)}) custom-call(bf16[512,512]{1,0:T(8,128)(2,1)} %get-tuple-element.37.high, bf16[512,512]{1,0:T(8,128)(2,1)} %get-tuple-element.38.low, f32[256,512]{1,0:T(8,128)} %get-tuple-element.45.top, f32[256,512]{1,0:T(8,128)} %get-tuple-element.46.bottom), custom_call_target="tpu_custom_call" | custom-call | flops 805306368 | bytes 4194304 | tf_op jit(solution)/shard_map/pallas_call | solution.py:23
  115.1 4.1 %shard_map.52 = (f32[256,512]{1,0:T(8,128)}, f32[256,512]{1,0:T(8,128)}) custom-call(s32[4,3]{1,0:T(4,128)} %copy-done.21, f32[256,512]{1,0:T(8,128)} %copy-done.15, f32[256,512]{1,0:T(8,128)} %get-tuple-element.45.top, f32[256,512]{1,0:T(8,128)} %get-tuple-element.46.bottom, f32[256,512]{1,0:T(8,128)} %collective-permute-done.19.after, f32[512,384]{1,0:T(8,128)} %copy-done), custom_call_target="tpu_custom_call" | custom-call | flops 603979776 | bytes 4194304 | tf_op jit(solution)/shard_map/pallas_call | solution.py:23
  119.2 2.7 %collective-permute-start.21 = (f32[256,512]{1,0:T(8,128)}, f32[256,512]{1,0:T(8,128)}, u32[]{:S(2)}, u32[]{:S(2)}) collective-permute-start(f32[256,512]{1,0:T(8,128)} %get-tuple-element.50.bottom), channel_id=1, source_target_pairs={{0,4},{4,1},{1,5},{5,2},{2,6},{6,3},{3,7},{7,11},{11,15},{15,10},{... | collective-permute-start | bytes 1572872 | tf_op jit(solution)/shard_map/ppermute | solution.py:132
  121.9 1.5 collective-permute-start.22
  123.6 3.3 %shard_map.53 = (f32[256,512]{1,0:T(8,128)}, f32[256,512]{1,0:T(8,128)}) custom-call(bf16[512,512]{1,0:T(8,128)(2,1)} %get-tuple-element.37.high, bf16[512,512]{1,0:T(8,128)(2,1)} %get-tuple-element.38.low, f32[256,512]{1,0:T(8,128)} %get-tuple-element.49.top, f32[256,512]{1,0:T(8,128)} %get-tuple-element.50.bottom), custom_call_target="tpu_custom_call" | custom-call | flops 805306368 | bytes 4194304 | tf_op jit(solution)/shard_map/pallas_call | solution.py:23
  126.9 1.6 collective-permute-start.20
  128.5 4.1 %shard_map.54 = (f32[256,512]{1,0:T(8,128)}, f32[256,512]{1,0:T(8,128)}) custom-call(s32[4,3]{1,0:T(4,128)} %copy-done.21, f32[256,512]{1,0:T(8,128)} %collective-permute-done.21.before, f32[256,512]{1,0:T(8,128)} %get-tuple-element.49.top, f32[256,512]{1,0:T(8,128)} %get-tuple-element.50.bottom, f32[256,512]{1,0:T(8,128)} %collective-permute-done.22.after, ...), custom_call_target="tpu_custom_call" | custom-call | flops 603979776 | bytes 4194304 | tf_op jit(solution)/shard_map/pallas_call | solution.py:23
  132.6 7.9 %collective-permute-start.24 = (f32[256,512]{1,0:T(8,128)}, f32[256,512]{1,0:T(8,128)}, u32[]{:S(2)}, u32[]{:S(2)}) collective-permute-start(f32[256,512]{1,0:T(8,128)} %get-tuple-element.54.bottom), channel_id=1, source_target_pairs={{0,4},{4,1},{1,5},{5,2},{2,6},{6,3},{3,7},{7,11},{11,15},{15,10},{... | collective-permute-start | bytes 1572872 | tf_op jit(solution)/shard_map/ppermute | solution.py:132
  141.9 3.3 %shard_map.55 = (f32[256,512]{1,0:T(8,128)}, f32[256,512]{1,0:T(8,128)}) custom-call(bf16[512,512]{1,0:T(8,128)(2,1)} %get-tuple-element.37.high, bf16[512,512]{1,0:T(8,128)(2,1)} %get-tuple-element.38.low, f32[256,512]{1,0:T(8,128)} %get-tuple-element.53.top, f32[256,512]{1,0:T(8,128)} %get-tuple-element.54.bottom), custom_call_target="tpu_custom_call" | custom-call | flops 805306368 | bytes 4194304 | tf_op jit(solution)/shard_map/pallas_call | solution.py:23
  147.4 4.9 %collective-permute-start.12 = (f32[3,64,512]{2,1,0:T(8,128)}, f32[3,64,512]{2,1,0:T(8,128)}, u32[]{:S(2)}, u32[]{:S(2)}) collective-permute-start(f32[3,64,512]{2,1,0:T(8,128)} %get-tuple-element.72), channel_id=1, source_target_pairs={{0,8},{1,9},{2,10},{3,11},{4,12},{5,13},{6,14},{7,15},{8,16},{9,17... | collective-permute-start | bytes 1179656 | tf_op jit(solution)/shard_map/ppermute | solution.py:132
  153.5 2.3 collective-permute-start.14
  155.8 4.0 %shard_map.56 = (f32[256,512]{1,0:T(8,128)}, f32[256,512]{1,0:T(8,128)}) custom-call(s32[4,3]{1,0:T(4,128)} %copy-done.21, f32[256,512]{1,0:T(8,128)} %collective-permute-done.24.before, f32[256,512]{1,0:T(8,128)} %get-tuple-element.53.top, f32[256,512]{1,0:T(8,128)} %get-tuple-element.54.bottom, f32[256,512]{1,0:T(8,128)} %collective-permute-done.25.after, ...), custom_call_target="tpu_custom_call" | custom-call | flops 603979776 | bytes 4194304 | tf_op jit(solution)/shard_map/pallas_call | solution.py:23
  159.9 3.4 %shard_map.57 = (f32[256,512]{1,0:T(8,128)}, f32[256,512]{1,0:T(8,128)}) custom-call(bf16[512,512]{1,0:T(8,128)(2,1)} %get-tuple-element.37.high, bf16[512,512]{1,0:T(8,128)(2,1)} %get-tuple-element.38.low, f32[256,512]{1,0:T(8,128)} %get-tuple-element.57.top, f32[256,512]{1,0:T(8,128)} %get-tuple-element.58.bottom), custom_call_target="tpu_custom_call" | custom-call | flops 805306368 | bytes 4194304 | tf_op jit(solution)/shard_map/pallas_call | solution.py:23
  163.4 2.5 collective-permute-start.33
  169.7 4.2 %collective-permute-start.27 = (f32[3,64,512]{2,1,0:T(8,128)}, f32[3,64,512]{2,1,0:T(8,128)}, u32[]{:S(2)}, u32[]{:S(2)}) collective-permute-start(f32[3,64,512]{2,1,0:T(8,128)} %get-tuple-element.69), channel_id=1, source_target_pairs={{0,8},{1,9},{2,10},{3,11},{4,12},{5,13},{6,14},{7,15},{8,16},{9,17... | collective-permute-start | bytes 1179656 | tf_op jit(solution)/shard_map/ppermute | solution.py:132
  173.9 5.8 %collective-permute-start.28 = (f32[3,64,512]{2,1,0:T(8,128)}, f32[3,64,512]{2,1,0:T(8,128)}, u32[]{:S(2)}, u32[]{:S(2)}) collective-permute-start(f32[3,64,512]{2,1,0:T(8,128)} %get-tuple-element.71), channel_id=1, source_target_pairs={{0,16},{1,17},{2,18},{3,19},{4,20},{5,21},{6,22},{7,23},{8,24},{9,... | collective-permute-start | bytes 1179656 | tf_op jit(solution)/shard_map/ppermute | solution.py:132
  180.6 4.0 %shard_map.58 = (f32[256,512]{1,0:T(8,128)}, f32[256,512]{1,0:T(8,128)}) custom-call(s32[4,3]{1,0:T(4,128)} %copy-done.21, f32[256,512]{1,0:T(8,128)} %copy-done.10, f32[256,512]{1,0:T(8,128)} %get-tuple-element.57.top, f32[256,512]{1,0:T(8,128)} %get-tuple-element.58.bottom, f32[256,512]{1,0:T(8,128)} %copy-done.14, f32[512,384]{1,0:T(8,128)} %copy-done), custom_call_target="tpu_custom_call" | custom-call | flops 603979776 | bytes 4194304 | tf_op jit(solution)/shard_map/pallas_call | solution.py:23
  184.6 3.3 %shard_map.59 = (f32[256,512]{1,0:T(8,128)}, f32[256,512]{1,0:T(8,128)}) custom-call(bf16[512,512]{1,0:T(8,128)(2,1)} %get-tuple-element.37.high, bf16[512,512]{1,0:T(8,128)(2,1)} %get-tuple-element.38.low, f32[256,512]{1,0:T(8,128)} %get-tuple-element.61.top, f32[256,512]{1,0:T(8,128)} %get-tuple-element.62.bottom), custom_call_target="tpu_custom_call" | custom-call | flops 805306368 | bytes 4194304 | tf_op jit(solution)/shard_map/pallas_call | solution.py:23
  187.9 1.4 fusion.3
  189.4 3.6 %collective-permute-start.15 = (f32[3,64,512]{2,1,0:T(8,128)S(1)}, f32[3,64,512]{2,1,0:T(8,128)S(1)}, u32[]{:S(2)}, u32[]{:S(2)}) collective-permute-start(f32[3,64,512]{2,1,0:T(8,128)S(1)} %fusion.3), channel_id=1, source_target_pairs={{0,1},{4,5},{8,9},{12,13},{16,17},{20,21},{24,25},{28,29},{3,2},{7... | collective-permute-start | bytes 1179656 | tf_op jit(solution)/shard_map/ppermute | solution.py:132
  194.1 1.4 fusion.1
  195.5 1.3 collective-permute-start.30
  197.0 7.7 %collective-permute-start.36 = (f32[1,64,512]{2,1,0:T(8,128)S(1)}, f32[1,64,512]{2,1,0:T(8,128)S(1)}, u32[]{:S(2)}, u32[]{:S(2)}) collective-permute-start(f32[1,64,512]{2,1,0:T(8,128)S(1)} %get-tuple-element.77), channel_id=1, source_target_pairs={{0,8},{1,9},{2,10},{3,11},{4,12},{5,13},{6,14},{7,15},{8,16},{9,17... | collective-permute-start | bytes 393224 | tf_op jit(solution)/shard_map/ppermute | solution.py:132
  204.7 1.5 collective-permute-start.38
  207.0 3.0 %collective-permute-done.30 = f32[3,64,512]{2,1,0:T(8,128)S(1)} collective-permute-done((f32[3,64,512]{2,1,0:T(8,128)S(1)}, f32[3,64,512]{2,1,0:T(8,128)S(1)}, u32[]{:S(2)}, u32[]{:S(2)}) %collective-permute-start.30) | collective-permute-done | bytes 393248 | tf_op jit(solution)/shard_map/ppermute | solution.py:132
  211.1 6.6 %collective-permute-start.39 = (f32[1,64,512]{2,1,0:T(8,128)S(1)}, f32[1,64,512]{2,1,0:T(8,128)S(1)}, u32[]{:S(2)}, u32[]{:S(2)}) collective-permute-start(f32[1,64,512]{2,1,0:T(8,128)S(1)} %fusion.5), channel_id=1, source_target_pairs={{0,1},{4,5},{8,9},{12,13},{16,17},{20,21},{24,25},{28,29}} | collective-permute-start | bytes 393224 | tf_op jit(solution)/shard_map/ppermute | solution.py:132
  217.7 2.5 collective-permute-done.39
  225.1 10.2 %collective-permute-done.17 = f32[3,64,512]{2,1,0:T(8,128)S(1)} collective-permute-done((f32[3,64,512]{2,1,0:T(8,128)S(1)}, f32[3,64,512]{2,1,0:T(8,128)S(1)}, u32[]{:S(2)}, u32[]{:S(2)}) %collective-permute-start.17) | collective-permute-done | bytes 393248 | tf_op jit(solution)/shard_map/ppermute | solution.py:132
  235.4 6.5 %collective-permute-done.32 = f32[3,64,512]{2,1,0:T(8,128)S(1)} collective-permute-done((f32[3,64,512]{2,1,0:T(8,128)S(1)}, f32[3,64,512]{2,1,0:T(8,128)S(1)}, u32[]{:S(2)}, u32[]{:S(2)}) %collective-permute-start.32) | collective-permute-done | bytes 393248 | tf_op jit(solution)/shard_map/ppermute | solution.py:132
  243.5 2.2 shard_map.60
  245.7 2.9 %collective-permute-start.42 = (f32[64,512]{1,0:T(8,128)}, f32[64,512]{1,0:T(8,128)S(1)}, u32[]{:S(2)}, u32[]{:S(2)}) collective-permute-start(f32[64,512]{1,0:T(8,128)} %get-tuple-element.66), channel_id=1, source_target_pairs={{0,8},{1,9},{2,10},{3,11},{4,12},{5,13},{6,14},{7,15},{8,16},{9,17... | collective-permute-start | bytes 393224 | tf_op jit(solution)/shard_map/ppermute | solution.py:132
  248.6 1.3 collective-permute-start.43
  250.0 2.8 %collective-permute-start.44 = (f32[64,512]{1,0:T(8,128)}, f32[64,512]{1,0:T(8,128)S(1)}, u32[]{:S(2)}, u32[]{:S(2)}) collective-permute-start(f32[64,512]{1,0:T(8,128)} %get-tuple-element.68), channel_id=1, source_target_pairs={{0,24},{1,25},{2,26},{3,27},{4,28},{5,29},{6,30},{7,31},{8,0},{9,1... | collective-permute-start | bytes 393224 | tf_op jit(solution)/shard_map/ppermute | solution.py:132
  254.5 1.4 collective-permute-done.44.refs_3_
  256.5 1.9 shard_map.61
  (133 shorter events, 31.4 us)
Async XLA Ops:
  1.3 2.1 collective-permute-start.2
  2.1 13.5 %collective-permute-start.1 = (f32[256,512]{1,0:T(8,128)S(1)}, f32[256,512]{1,0:T(8,128)S(1)}, u32[]{:S(2)}, u32[]{:S(2)}) collective-permute-start(f32[256,512]{1,0:T(8,128)S(1)} %get-tuple-element.75), channel_id=1, source_target_pairs={{0,0},{1,4},{2,1},{3,5},{4,2},{5,6},{6,3},{7,7},{8,11},{9,15},{10,... | collective-permute-start | bytes 1572872 | tf_op jit(solution)/shard_map/ppermute | solution.py:132
  2.8 16.7 %collective-permute-start.7 = (f32[512,384]{1,0:T(8,128)S(1)}, f32[512,384]{1,0:T(8,128)S(1)}, u32[]{:S(2)}, u32[]{:S(2)}) collective-permute-start(f32[512,384]{1,0:T(8,128)S(1)} %copy-done.22), channel_id=1, source_target_pairs={{0,0},{1,4},{2,1},{3,5},{4,2},{5,6},{6,3},{7,7},{8,11},{9,15},{10,... | collective-permute-start | bytes 2359304 | tf_op jit(solution)/shard_map/ppermute | solution.py:132
  3.5 37.1 %copy-start.2 = (f32[256,512]{1,0:T(8,128)}, f32[256,512]{1,0:T(8,128)S(1)}, u32[]{:S(2)}) copy-start(f32[256,512]{1,0:T(8,128)S(1)} %collective-permute-done.2.bottom) | copy-start | bytes 1572868
  3.5 15.9 %collective-permute-start.5 = (f32[256,512]{1,0:T(8,128)S(1)}, f32[256,512]{1,0:T(8,128)S(1)}, u32[]{:S(2)}, u32[]{:S(2)}) collective-permute-start(f32[256,512]{1,0:T(8,128)S(1)} %collective-permute-done.2.bottom), channel_id=1, source_target_pairs={{0,4},{4,1},{1,5},{5,2},{2,6},{6,3},{3,7},{7,11},{11,15},{15,10},{... | collective-permute-start | bytes 1572872 | tf_op jit(solution)/shard_map/ppermute | solution.py:132
  15.5 25.1 %copy-start.3 = (f32[256,512]{1,0:T(8,128)}, f32[256,512]{1,0:T(8,128)S(1)}, u32[]{:S(2)}) copy-start(f32[256,512]{1,0:T(8,128)S(1)} %collective-permute-done.1.top) | copy-start | bytes 1572868
  15.6 25.1 %collective-permute-start.6 = (f32[256,512]{1,0:T(8,128)S(1)}, f32[256,512]{1,0:T(8,128)}, u32[]{:S(2)}, u32[]{:S(2)}) collective-permute-start(f32[256,512]{1,0:T(8,128)S(1)} %collective-permute-done.1.top), channel_id=1, source_target_pairs={{4,0},{1,4},{5,1},{2,5},{6,2},{3,6},{7,3},{11,7},{15,11},{10,15},{... | collective-permute-start | bytes 1572872 | tf_op jit(solution)/shard_map/ppermute | solution.py:132
  16.9 53.6 %collective-permute-start = (f32[512,512]{1,0:T(8,128)}, f32[512,512]{1,0:T(8,128)S(1)}, u32[]{:S(2)}, u32[]{:S(2)}) collective-permute-start(f32[512,512]{1,0:T(8,128)} %param.5), channel_id=1, source_target_pairs={{0,0},{1,4},{2,1},{3,5},{4,2},{5,6},{6,3},{7,7},{8,11},{9,15},{10,... | collective-permute-start | bytes 3145736 | tf_op jit(solution)/shard_map/ppermute | solution.py:132
  18.7 0.7 collective-permute-start.4
  19.4 21.2 %copy-start.21 = (s32[4,3]{1,0:T(4,128)}, s32[4,3]{1,0:T(4,128)S(1)}, u32[]{:S(2)}) copy-start(s32[4,3]{1,0:T(4,128)S(1)} %collective-permute-done.4.offs) | copy-start | bytes 148
  44.7 30.3 %collective-permute-start.10 = (f32[256,512]{1,0:T(8,128)}, f32[256,512]{1,0:T(8,128)S(1)}, u32[]{:S(2)}, u32[]{:S(2)}) collective-permute-start(f32[256,512]{1,0:T(8,128)} %get-tuple-element.41.top), channel_id=1, source_target_pairs={{4,0},{1,4},{5,1},{2,5},{6,2},{3,6},{7,3},{11,7},{15,11},{10,15},{... | collective-permute-start | bytes 1572872 | tf_op jit(solution)/shard_map/ppermute | solution.py:132
  46.0 29.0 %collective-permute-start.9 = (f32[256,512]{1,0:T(8,128)}, f32[256,512]{1,0:T(8,128)S(1)}, u32[]{:S(2)}, u32[]{:S(2)}) collective-permute-start(f32[256,512]{1,0:T(8,128)} %get-tuple-element.42.bottom), channel_id=1, source_target_pairs={{0,4},{4,1},{1,5},{5,2},{2,6},{6,3},{3,7},{7,11},{11,15},{15,10},{... | collective-permute-start | bytes 1572872 | tf_op jit(solution)/shard_map/ppermute | solution.py:132
  80.7 33.7 %collective-permute-start.18 = (f32[256,512]{1,0:T(8,128)}, f32[256,512]{1,0:T(8,128)S(1)}, u32[]{:S(2)}, u32[]{:S(2)}) collective-permute-start(f32[256,512]{1,0:T(8,128)} %get-tuple-element.46.bottom), channel_id=1, source_target_pairs={{0,4},{4,1},{1,5},{5,2},{2,6},{6,3},{3,7},{7,11},{11,15},{15,10},{... | collective-permute-start | bytes 1572872 | tf_op jit(solution)/shard_map/ppermute | solution.py:132
  99.6 14.8 %collective-permute-start.19 = (f32[256,512]{1,0:T(8,128)}, f32[256,512]{1,0:T(8,128)}, u32[]{:S(2)}, u32[]{:S(2)}) collective-permute-start(f32[256,512]{1,0:T(8,128)} %get-tuple-element.45.top), channel_id=1, source_target_pairs={{4,0},{1,4},{5,1},{2,5},{6,2},{3,6},{7,3},{11,7},{15,11},{10,15},{... | collective-permute-start | bytes 1572872 | tf_op jit(solution)/shard_map/ppermute | solution.py:132
  104.2 19.2 %collective-permute-start.8 = (f32[256,512]{1,0:T(8,128)}, f32[256,512]{1,0:T(8,128)S(1)}, u32[]{:S(2)}, u32[]{:S(2)}) collective-permute-start(f32[256,512]{1,0:T(8,128)} %get-tuple-element.44), channel_id=1, source_target_pairs={{0,4},{1,5},{2,6},{3,7},{4,0},{5,1},{6,2},{7,3},{8,12},{9,13},{10,... | collective-permute-start | bytes 1572872 | tf_op jit(solution)/shard_map/ppermute | solution.py:132
  110.5 13.0 %collective-permute-start.3 = (f32[256,512]{1,0:T(8,128)}, f32[256,512]{1,0:T(8,128)S(1)}, u32[]{:S(2)}, u32[]{:S(2)}) collective-permute-start(f32[256,512]{1,0:T(8,128)} %get-tuple-element.40), channel_id=1, source_target_pairs={{0,4},{1,5},{2,6},{3,7},{4,0},{5,1},{6,2},{7,3},{8,12},{9,13},{10,... | collective-permute-start | bytes 1572872 | tf_op jit(solution)/shard_map/ppermute | solution.py:132
  113.8 27.9 %collective-permute-start.11 = (f32[256,512]{1,0:T(8,128)}, f32[256,512]{1,0:T(8,128)S(1)}, u32[]{:S(2)}, u32[]{:S(2)}) collective-permute-start(f32[256,512]{1,0:T(8,128)} %get-tuple-element.48), channel_id=1, source_target_pairs={{0,4},{1,5},{2,6},{3,7},{4,0},{5,1},{6,2},{7,3},{8,12},{9,13},{10,... | collective-permute-start | bytes 1572872 | tf_op jit(solution)/shard_map/ppermute | solution.py:132
  119.2 9.3 %collective-permute-start.21 = (f32[256,512]{1,0:T(8,128)}, f32[256,512]{1,0:T(8,128)}, u32[]{:S(2)}, u32[]{:S(2)}) collective-permute-start(f32[256,512]{1,0:T(8,128)} %get-tuple-element.50.bottom), channel_id=1, source_target_pairs={{0,4},{4,1},{1,5},{5,2},{2,6},{6,3},{3,7},{7,11},{11,15},{15,10},{... | collective-permute-start | bytes 1572872 | tf_op jit(solution)/shard_map/ppermute | solution.py:132
  121.9 6.6 %collective-permute-start.22 = (f32[256,512]{1,0:T(8,128)}, f32[256,512]{1,0:T(8,128)}, u32[]{:S(2)}, u32[]{:S(2)}) collective-permute-start(f32[256,512]{1,0:T(8,128)} %get-tuple-element.49.top), channel_id=1, source_target_pairs={{4,0},{1,4},{5,1},{2,5},{6,2},{3,6},{7,3},{11,7},{15,11},{10,15},{... | collective-permute-start | bytes 1572872 | tf_op jit(solution)/shard_map/ppermute | solution.py:132
  126.9 36.4 %collective-permute-start.20 = (f32[256,512]{1,0:T(8,128)}, f32[256,512]{1,0:T(8,128)S(1)}, u32[]{:S(2)}, u32[]{:S(2)}) collective-permute-start(f32[256,512]{1,0:T(8,128)} %get-tuple-element.52), channel_id=1, source_target_pairs={{0,4},{1,5},{2,6},{3,7},{4,0},{5,1},{6,2},{7,3},{8,12},{9,13},{10,... | collective-permute-start | bytes 1572872 | tf_op jit(solution)/shard_map/ppermute | solution.py:132
  132.6 19.8 %collective-permute-start.24 = (f32[256,512]{1,0:T(8,128)}, f32[256,512]{1,0:T(8,128)}, u32[]{:S(2)}, u32[]{:S(2)}) collective-permute-start(f32[256,512]{1,0:T(8,128)} %get-tuple-element.54.bottom), channel_id=1, source_target_pairs={{0,4},{4,1},{1,5},{5,2},{2,6},{6,3},{3,7},{7,11},{11,15},{15,10},{... | collective-permute-start | bytes 1572872 | tf_op jit(solution)/shard_map/ppermute | solution.py:132
  140.4 13.1 %collective-permute-start.25 = (f32[256,512]{1,0:T(8,128)}, f32[256,512]{1,0:T(8,128)}, u32[]{:S(2)}, u32[]{:S(2)}) collective-permute-start(f32[256,512]{1,0:T(8,128)} %get-tuple-element.53.top), channel_id=1, source_target_pairs={{4,0},{1,4},{5,1},{2,5},{6,2},{3,6},{7,3},{11,7},{15,11},{10,15},{... | collective-permute-start | bytes 1572872 | tf_op jit(solution)/shard_map/ppermute | solution.py:132
  145.3 18.2 %collective-permute-start.23 = (f32[256,512]{1,0:T(8,128)}, f32[256,512]{1,0:T(8,128)}, u32[]{:S(2)}, u32[]{:S(2)}) collective-permute-start(f32[256,512]{1,0:T(8,128)} %get-tuple-element.56), channel_id=1, source_target_pairs={{0,4},{1,5},{2,6},{3,7},{4,0},{5,1},{6,2},{7,3},{8,12},{9,13},{10,... | collective-permute-start | bytes 1572872 | tf_op jit(solution)/shard_map/ppermute | solution.py:132
  147.4 22.3 %collective-permute-start.12 = (f32[3,64,512]{2,1,0:T(8,128)}, f32[3,64,512]{2,1,0:T(8,128)}, u32[]{:S(2)}, u32[]{:S(2)}) collective-permute-start(f32[3,64,512]{2,1,0:T(8,128)} %get-tuple-element.72), channel_id=1, source_target_pairs={{0,8},{1,9},{2,10},{3,11},{4,12},{5,13},{6,14},{7,15},{8,16},{9,17... | collective-permute-start | bytes 1179656 | tf_op jit(solution)/shard_map/ppermute | solution.py:132
  152.3 35.6 %collective-permute-start.13 = (f32[3,64,512]{2,1,0:T(8,128)}, f32[3,64,512]{2,1,0:T(8,128)}, u32[]{:S(2)}, u32[]{:S(2)}) collective-permute-start(f32[3,64,512]{2,1,0:T(8,128)} %get-tuple-element.74), channel_id=1, source_target_pairs={{0,16},{1,17},{2,18},{3,19},{4,20},{5,21},{6,22},{7,23},{8,24},{9,... | collective-permute-start | bytes 1179656 | tf_op jit(solution)/shard_map/ppermute | solution.py:132
  153.5 34.4 %collective-permute-start.14 = (f32[3,64,512]{2,1,0:T(8,128)S(1)}, f32[3,64,512]{2,1,0:T(8,128)}, u32[]{:S(2)}, u32[]{:S(2)}) collective-permute-start(f32[3,64,512]{2,1,0:T(8,128)S(1)} %get-tuple-element.73), channel_id=1, source_target_pairs={{0,24},{1,25},{2,26},{3,27},{4,28},{5,29},{6,30},{7,31},{8,0},{9,1... | collective-permute-start | bytes 1179656 | tf_op jit(solution)/shard_map/ppermute | solution.py:132
  163.3 3.8 %collective-permute-start.26 = (f32[256,512]{1,0:T(8,128)}, f32[256,512]{1,0:T(8,128)S(1)}, u32[]{:S(2)}, u32[]{:S(2)}) collective-permute-start(f32[256,512]{1,0:T(8,128)} %get-tuple-element.60), channel_id=1, source_target_pairs={{0,4},{1,5},{2,6},{3,7},{4,0},{5,1},{6,2},{7,3},{8,12},{9,13},{10,... | collective-permute-start | bytes 1572872 | tf_op jit(solution)/shard_map/ppermute | solution.py:132
  163.4 10.5 %collective-permute-start.33 = (f32[256,512]{1,0:T(8,128)}, f32[256,512]{1,0:T(8,128)S(1)}, u32[]{:S(2)}, u32[]{:S(2)}) collective-permute-start(f32[256,512]{1,0:T(8,128)} %get-tuple-element.58.bottom), channel_id=1, source_target_pairs={{0,4},{4,1},{1,5},{5,2},{2,6},{6,3},{3,7},{7,11},{11,15},{15,10},{... | collective-permute-start | bytes 1572872 | tf_op jit(solution)/shard_map/ppermute | solution.py:132
  167.2 12.6 %collective-permute-start.34 = (f32[256,512]{1,0:T(8,128)S(1)}, f32[256,512]{1,0:T(8,128)S(1)}, u32[]{:S(2)}, u32[]{:S(2)}) collective-permute-start(f32[256,512]{1,0:T(8,128)S(1)} %copy-done.5), channel_id=1, source_target_pairs={{4,0},{1,4},{5,1},{2,5},{6,2},{3,6},{7,3},{11,7},{15,11},{10,15},{... | collective-permute-start | bytes 1572872 | tf_op jit(solution)/shard_map/ppermute | solution.py:132
  169.7 23.3 %collective-permute-start.27 = (f32[3,64,512]{2,1,0:T(8,128)}, f32[3,64,512]{2,1,0:T(8,128)}, u32[]{:S(2)}, u32[]{:S(2)}) collective-permute-start(f32[3,64,512]{2,1,0:T(8,128)} %get-tuple-element.69), channel_id=1, source_target_pairs={{0,8},{1,9},{2,10},{3,11},{4,12},{5,13},{6,14},{7,15},{8,16},{9,17... | collective-permute-start | bytes 1179656 | tf_op jit(solution)/shard_map/ppermute | solution.py:132
  173.9 20.2 %collective-permute-start.28 = (f32[3,64,512]{2,1,0:T(8,128)}, f32[3,64,512]{2,1,0:T(8,128)}, u32[]{:S(2)}, u32[]{:S(2)}) collective-permute-start(f32[3,64,512]{2,1,0:T(8,128)} %get-tuple-element.71), channel_id=1, source_target_pairs={{0,16},{1,17},{2,18},{3,19},{4,20},{5,21},{6,22},{7,23},{8,24},{9,... | collective-permute-start | bytes 1179656 | tf_op jit(solution)/shard_map/ppermute | solution.py:132
  180.6 13.5 %collective-permute-start.29 = (f32[3,64,512]{2,1,0:T(8,128)}, f32[3,64,512]{2,1,0:T(8,128)}, u32[]{:S(2)}, u32[]{:S(2)}) collective-permute-start(f32[3,64,512]{2,1,0:T(8,128)} %get-tuple-element.70), channel_id=1, source_target_pairs={{0,24},{1,25},{2,26},{3,27},{4,28},{5,29},{6,30},{7,31},{8,0},{9,1... | collective-permute-start | bytes 1179656 | tf_op jit(solution)/shard_map/ppermute | solution.py:132
  187.9 8.9 %collective-permute-start.35 = (f32[256,512]{1,0:T(8,128)}, f32[256,512]{1,0:T(8,128)S(1)}, u32[]{:S(2)}, u32[]{:S(2)}) collective-permute-start(f32[256,512]{1,0:T(8,128)} %get-tuple-element.64), channel_id=1, source_target_pairs={{0,4},{1,5},{2,6},{3,7},{4,0},{5,1},{6,2},{7,3},{8,12},{9,13},{10,... | collective-permute-start | bytes 1572872 | tf_op jit(solution)/shard_map/ppermute | solution.py:132
  189.4 16.9 %collective-permute-start.15 = (f32[3,64,512]{2,1,0:T(8,128)S(1)}, f32[3,64,512]{2,1,0:T(8,128)S(1)}, u32[]{:S(2)}, u32[]{:S(2)}) collective-permute-start(f32[3,64,512]{2,1,0:T(8,128)S(1)} %fusion.3), channel_id=1, source_target_pairs={{0,1},{4,5},{8,9},{12,13},{16,17},{20,21},{24,25},{28,29},{3,2},{7... | collective-permute-start | bytes 1179656 | tf_op jit(solution)/shard_map/ppermute | solution.py:132
  195.5 14.5 %collective-permute-start.30 = (f32[3,64,512]{2,1,0:T(8,128)S(1)}, f32[3,64,512]{2,1,0:T(8,128)S(1)}, u32[]{:S(2)}, u32[]{:S(2)}) collective-permute-start(f32[3,64,512]{2,1,0:T(8,128)S(1)} %fusion.1), channel_id=1, source_target_pairs={{0,1},{4,5},{8,9},{12,13},{16,17},{20,21},{24,25},{28,29},{3,2},{7... | collective-permute-start | bytes 1179656 | tf_op jit(solution)/shard_map/ppermute | solution.py:132
  197.0 13.8 %collective-permute-start.36 = (f32[1,64,512]{2,1,0:T(8,128)S(1)}, f32[1,64,512]{2,1,0:T(8,128)S(1)}, u32[]{:S(2)}, u32[]{:S(2)}) collective-permute-start(f32[1,64,512]{2,1,0:T(8,128)S(1)} %get-tuple-element.77), channel_id=1, source_target_pairs={{0,8},{1,9},{2,10},{3,11},{4,12},{5,13},{6,14},{7,15},{8,16},{9,17... | collective-permute-start | bytes 393224 | tf_op jit(solution)/shard_map/ppermute | solution.py:132
  204.7 6.0 %collective-permute-start.37 = (f32[1,64,512]{2,1,0:T(8,128)S(1)}, f32[1,64,512]{2,1,0:T(8,128)S(1)}, u32[]{:S(2)}, u32[]{:S(2)}) collective-permute-start(f32[1,64,512]{2,1,0:T(8,128)S(1)} %get-tuple-element.79), channel_id=1, source_target_pairs={{0,16},{1,17},{2,18},{3,19},{4,20},{5,21},{6,22},{7,23},{8,24},{9,... | collective-permute-start | bytes 393224 | tf_op jit(solution)/shard_map/ppermute | solution.py:132
  204.7 6.4 %collective-permute-start.38 = (f32[1,64,512]{2,1,0:T(8,128)S(1)}, f32[1,64,512]{2,1,0:T(8,128)S(1)}, u32[]{:S(2)}, u32[]{:S(2)}) collective-permute-start(f32[1,64,512]{2,1,0:T(8,128)S(1)} %get-tuple-element.78), channel_id=1, source_target_pairs={{0,24},{1,25},{2,26},{3,27},{4,28},{5,29},{6,30},{7,31},{8,0},{9,1... | collective-permute-start | bytes 393224 | tf_op jit(solution)/shard_map/ppermute | solution.py:132
  206.3 14.6 %collective-permute-start.16 = (f32[3,64,512]{2,1,0:T(8,128)S(1)}, f32[3,64,512]{2,1,0:T(8,128)S(1)}, u32[]{:S(2)}, u32[]{:S(2)}) collective-permute-start(f32[3,64,512]{2,1,0:T(8,128)S(1)} %add.83), channel_id=1, source_target_pairs={{1,2},{5,6},{9,10},{13,14},{17,18},{21,22},{25,26},{29,30},{2,1},{... | collective-permute-start | bytes 1179656 | tf_op jit(solution)/shard_map/ppermute | solution.py:132
  210.0 12.3 %collective-permute-start.31 = (f32[3,64,512]{2,1,0:T(8,128)S(1)}, f32[3,64,512]{2,1,0:T(8,128)S(1)}, u32[]{:S(2)}, u32[]{:S(2)}) collective-permute-start(f32[3,64,512]{2,1,0:T(8,128)S(1)} %add.91), channel_id=1, source_target_pairs={{1,2},{5,6},{9,10},{13,14},{17,18},{21,22},{25,26},{29,30},{2,1},{... | collective-permute-start | bytes 1179656 | tf_op jit(solution)/shard_map/ppermute | solution.py:132
  211.1 9.1 %collective-permute-start.39 = (f32[1,64,512]{2,1,0:T(8,128)S(1)}, f32[1,64,512]{2,1,0:T(8,128)S(1)}, u32[]{:S(2)}, u32[]{:S(2)}) collective-permute-start(f32[1,64,512]{2,1,0:T(8,128)S(1)} %fusion.5), channel_id=1, source_target_pairs={{0,1},{4,5},{8,9},{12,13},{16,17},{20,21},{24,25},{28,29}} | collective-permute-start | bytes 393224 | tf_op jit(solution)/shard_map/ppermute | solution.py:132
  220.3 3.4 %collective-permute-start.40 = (f32[1,64,512]{2,1,0:T(8,128)S(1)}, f32[1,64,512]{2,1,0:T(8,128)S(1)}, u32[]{:S(2)}, u32[]{:S(2)}) collective-permute-start(f32[1,64,512]{2,1,0:T(8,128)S(1)} %add.97), channel_id=1, source_target_pairs={{1,2},{5,6},{9,10},{13,14},{17,18},{21,22},{25,26},{29,30}} | collective-permute-start | bytes 393224 | tf_op jit(solution)/shard_map/ppermute | solution.py:132
  221.0 14.3 %collective-permute-start.17 = (f32[3,64,512]{2,1,0:T(8,128)S(1)}, f32[3,64,512]{2,1,0:T(8,128)S(1)}, u32[]{:S(2)}, u32[]{:S(2)}) collective-permute-start(f32[3,64,512]{2,1,0:T(8,128)S(1)} %add.84), channel_id=1, source_target_pairs={{1,0},{5,4},{9,8},{13,12},{17,16},{21,20},{25,24},{29,28}} | collective-permute-start | bytes 1179656 | tf_op jit(solution)/shard_map/ppermute | solution.py:132
  222.4 19.4 %collective-permute-start.32 = (f32[3,64,512]{2,1,0:T(8,128)S(1)}, f32[3,64,512]{2,1,0:T(8,128)S(1)}, u32[]{:S(2)}, u32[]{:S(2)}) collective-permute-start(f32[3,64,512]{2,1,0:T(8,128)S(1)} %add.92), channel_id=1, source_target_pairs={{1,0},{5,4},{9,8},{13,12},{17,16},{21,20},{25,24},{29,28},{2,3},{6... | collective-permute-start | bytes 1179656 | tf_op jit(solution)/shard_map/ppermute | solution.py:132
  223.7 0.7 collective-permute-start.41
  245.7 8.1 %collective-permute-start.42 = (f32[64,512]{1,0:T(8,128)}, f32[64,512]{1,0:T(8,128)S(1)}, u32[]{:S(2)}, u32[]{:S(2)}) collective-permute-start(f32[64,512]{1,0:T(8,128)} %get-tuple-element.66), channel_id=1, source_target_pairs={{0,8},{1,9},{2,10},{3,11},{4,12},{5,13},{6,14},{7,15},{8,16},{9,17... | collective-permute-start | bytes 393224 | tf_op jit(solution)/shard_map/ppermute | solution.py:132
  248.6 5.9 %collective-permute-start.43 = (f32[64,512]{1,0:T(8,128)}, f32[64,512]{1,0:T(8,128)S(1)}, u32[]{:S(2)}, u32[]{:S(2)}) collective-permute-start(f32[64,512]{1,0:T(8,128)} %get-tuple-element.67), channel_id=1, source_target_pairs={{0,16},{1,17},{2,18},{3,19},{4,20},{5,21},{6,22},{7,23},{8,24},{9,... | collective-permute-start | bytes 393224 | tf_op jit(solution)/shard_map/ppermute | solution.py:132
  250.0 5.9 %collective-permute-start.44 = (f32[64,512]{1,0:T(8,128)}, f32[64,512]{1,0:T(8,128)S(1)}, u32[]{:S(2)}, u32[]{:S(2)}) collective-permute-start(f32[64,512]{1,0:T(8,128)} %get-tuple-element.68), channel_id=1, source_target_pairs={{0,24},{1,25},{2,26},{3,27},{4,28},{5,29},{6,30},{7,31},{8,0},{9,1... | collective-permute-start | bytes 393224 | tf_op jit(solution)/shard_map/ppermute | solution.py:132
  (21 other events, 139.5 us)
